TPU v7x, 32 devices: a whole 2x2x4 slice. The times are simulated.
32 devices in a mesh: ctx: 16 (over z, y, x), tp: 2 (over core).
Axes of the slice: x: 2, y: 2, z: 4, core: 2. Of those that a mesh axis runs over, the one named last changes fastest.
Arguments:
- hidden_states: bfloat16 [4096, 8192], P('ctx', 'tp'), may hold values from -6 to 6
- queries: bfloat16 [4096, 4096], P('ctx', 'tp')
- key_matrix: bfloat16 [8192, 1024], P('tp'), may hold values from -0.0625 to 0.0625
- value_matrix: bfloat16 [8192, 1024], P('tp'), may hold values from -0.0625 to 0.0625
- stretch_table: int32 [32], replicated, may hold values from 0 to 31, as said below
Outputs:
- attended: bfloat16 [4096, 4096], P('ctx', 'tp')
Inputs may be any that keep to these rules, and one draw needn't show every extreme that they name: `stretch_table`: a permutation of 0 to 31 in which entries 2 i and 2 i + 1 are two stretches c and 31 - c.
All inputs are finite; a program needn't handle non-finite values.
Results may differ from a plain program's by a relative error of at most 0.007.
The roundings to bfloat16 on the way count: a program that leaves them out, or rounds other values in their place, can miss the bound.
Values may be sent and summed in bfloat16 or wider, within the bound.
A program may use at most 256 MiB of HBM per device.

v0:
```python
import math

import jax
import jax.numpy as jnp
from jax import lax
from jax.sharding import PartitionSpec as P

KEY_VALUE_HEADS = 8
HEAD_SIZE = 128


def stretch_position(stretch_ids, stretch_table):
    listed = jnp.arange(stretch_table.shape[0], dtype=jnp.int32)
    onehot = stretch_ids[:, None] == listed[None, :]
    return jnp.sum(jnp.where(onehot, stretch_table[None, :], 0), axis=1)


def body(hidden_states, queries, key_matrix, value_matrix, stretch_table):
    tokens_dev = hidden_states.shape[0]
    key_tiles = key_matrix.reshape(key_matrix.shape[0], KEY_VALUE_HEADS, HEAD_SIZE)
    value_tiles = value_matrix.reshape(value_matrix.shape[0], KEY_VALUE_HEADS, HEAD_SIZE)
    head_group = KEY_VALUE_HEADS // lax.axis_size("tp")
    key_term = jnp.einsum(
        "tc,chd->htd", hidden_states, key_tiles, preferred_element_type=jnp.float32
    )
    value_term = jnp.einsum(
        "tc,chd->htd", hidden_states, value_tiles, preferred_element_type=jnp.float32
    )
    shares = lax.psum_scatter(
        jnp.stack([key_term, value_term], axis=1), "tp", scatter_dimension=0, tiled=True
    )
    kv_local = shares.astype(jnp.bfloat16).transpose(2, 0, 1, 3)
    stretch = tokens_dev // 2
    ctx_size = lax.axis_size("ctx")
    all_rows = jnp.arange(ctx_size * tokens_dev, dtype=jnp.int32)
    all_places = stretch_position(all_rows // stretch, stretch_table) * stretch + all_rows % stretch
    device = lax.axis_index("ctx")
    query_place = lax.dynamic_slice_in_dim(all_places, device * tokens_dev, tokens_dev, 0)
    query_heads = queries.shape[1] // HEAD_SIZE
    group_ratio = query_heads // head_group
    query_grid = queries.reshape(tokens_dev, head_group, group_ratio, HEAD_SIZE)
    scale = 1.0 / HEAD_SIZE**0.5
    span_queries = (query_grid[:stretch], query_grid[stretch:])
    span_places = (query_place[:stretch], query_place[stretch:])
    span_latest = (jnp.max(span_places[0]), jnp.max(span_places[1]))

    def fresh():
        return (
            jnp.full((head_group, group_ratio, stretch), -1e30, jnp.float32),
            jnp.zeros((head_group, group_ratio, stretch), jnp.float32),
            jnp.zeros((head_group, group_ratio, stretch, HEAD_SIZE), jnp.float32),
        )

    carry = (fresh(), fresh())
    piece = lax.all_gather(kv_local, "ctx", axis=0, tiled=True)
    rows = piece.shape[0]
    width = math.gcd(rows, 1024)
    blocks = rows // width

    def visit(state, index):
        begin = index * width
        block = lax.dynamic_slice_in_dim(piece, begin, width, 0)
        key_place = lax.dynamic_slice_in_dim(all_places, begin, width, 0)
        earliest = jnp.min(key_place)
        key_block = block[:, :, 0]
        value_block = block[:, :, 1]
        updated = []
        for span in range(2):
            span_grid = span_queries[span]
            places = span_places[span]

            def attend(inner, span_grid=span_grid, places=places):
                highs, sums, partial_value = inner
                score = (
                    jnp.einsum(
                        "tgrd,ngd->grtn", span_grid, key_block, preferred_element_type=jnp.float32
                    )
                    * scale
                )
                visible = key_place[None, :] <= places[:, None]
                masked = jnp.where(visible, score, jnp.float32(-1e30))
                new_high = jnp.maximum(highs, jnp.max(masked, axis=-1))
                weight = jnp.where(visible, jnp.exp(masked - new_high[..., None]), jnp.float32(0.0))
                factor = jnp.exp(highs - new_high)
                sums = sums * factor + jnp.sum(weight, axis=-1)
                update = jnp.einsum(
                    "grtn,ngd->grtd",
                    weight.astype(jnp.bfloat16),
                    value_block,
                    preferred_element_type=jnp.float32,
                )
                partial_value = partial_value * factor[..., None] + update
                return (new_high, sums, partial_value)

            def keep_state(inner):
                return inner

            updated.append(lax.cond(earliest <= span_latest[span], attend, keep_state, state[span]))
        return ((updated[0], updated[1]), None)

    carry, _ = lax.scan(visit, carry, jnp.arange(blocks, dtype=jnp.int32))
    output = jnp.concatenate(
        [carry[0][2] / carry[0][1][..., None], carry[1][2] / carry[1][1][..., None]], axis=2
    )
    return (
        output.transpose(2, 0, 1, 3)
        .reshape(tokens_dev, query_heads * HEAD_SIZE)
        .astype(jnp.bfloat16)
    )


def solution(mesh):
    in_specs = (P("ctx", "tp"), P("ctx", "tp"), P("tp", None), P("tp", None), P())
    out_specs = P("ctx", "tp")
    return jax.shard_map(body, mesh=mesh, in_specs=in_specs, out_specs=out_specs, check_vma=False)
```

profile of v0, /device:TPU:0, one launch (start us, length us, event | category | flops | bytes accessed | tf_op | source)
XLA Modules:
  0.0 294.3 jit_solution(8657823326039178736)
XLA Ops:
  6.5 11.7 %copy.48 = bf16[4096,1024]{0,1:T(8,128)(2,1)} copy(bf16[4096,1024]{1,0:T(8,128)(2,1)} %param.13) | data formatting | bytes 16777216 | tf_op jit(solution)/shard_map/reshape | solution.py:20
  18.2 11.3 %copy.49 = bf16[4096,1024]{0,1:T(8,128)(2,1)} copy(bf16[4096,1024]{1,0:T(8,128)(2,1)} %param.14) | data formatting | bytes 16777216 | tf_op jit(solution)/shard_map/reshape | solution.py:21
  29.6 5.9 %fusion.34 = f32[8,1,256,128]{2,3,0,1:T(8,128)S(1)} fusion(bf16[4096,8,128]{0,2,1:T(8,128)(2,1)} %bitcast.116, bf16[256,4096]{1,0:T(8,128)(2,1)S(1)} %copy-done), kind=kOutput, calls=%fused_computation.41 | convolution fusion | flops 2147483648 | bytes 11534336 | tf_op jit(solution)/shard_map/tc,chd->htd/dot_general | solution.py:23
  35.5 2.4 fusion.37
  38.1 9.3 %all-reduce.2 = bf16[8,2,256,128]{2,3,0,1:T(8,128)(2,1)S(1)} all-reduce(f32[8,2,256,128]{2,3,0,1:T(8,128)S(1)} %pad_maximum_fusion), channel_id=2, replica_groups=mesh['ctx'=16,'tp'=2] {'tp'}, use_global_device_ids=true, to_apply=%region_0.0.clone | all-reduce | flops 524288 | bytes 3145728
  49.5 1.3 fusion.50
  54.3 132.2 %all-gather.2.cloned.1.call-done = bf16[4096,4,2,128]{0,3,1,2:T(8,128)(2,1)} async-done(((bf16[256,4,2,128]{0,3,1,2:T(8,128)(2,1)}), bf16[4096,4,2,128]{0,3,1,2:T(8,128)(2,1)}) %all-gather.2.cloned.1.call-update) | async-done | bytes 8388624 | tf_op jit(solution)/shard_map/all_gather | solution.py:55
  186.6 1.1 broadcast.66.clone
  187.7 1.1 broadcast.66
  188.8 94.1 %while.20 = (s32[]{:T(128)}, f32[4,4,128]{2,1,0:T(4,128)S(1)}, f32[4,4,128]{2,1,0:T(4,128)S(1)}, f32[4,4,128,128]{3,2,1,0:T(8,128)}, f32[4,4,128]{2,1,0:T(4,128)...) while((s32[]{:T(128)}, f32[4,4,128]{2,1,0:T(4,128)S(1)}, ...), condition=%wide.region_14.15_spmd, body=%wide.region_4.14_spmd.sunk | while | flops 2203329536 | bytes 88360624 | solution.py:101
  192.9 1.8 constant_dynamic-slice_fusion.3
  196.1 8.7 %conditional.4 = ((f32[4,4,128]{2,1,0:T(4,128)S(1)}, f32[4,4,128]{2,1,0:T(4,128)S(1)}, f32[4,4,128,128]{3,2,1,0:T(8,128)})) conditional(s32[]{:T(128)} %convert_element_type.38, (f32[4,4,128]{2,1,0:T(4,128)S(1)}, f32[4,4,128]{2,1,0:T(4,128)S(1)}, f32[4,4,128,128]{3,2,1,0:T(8,128)}) %tuple.57, (s32[1024]{0:T(1024)S(1)}, s32[128]{0:T(128)S(1)}, ...), branch_computations={%region_6.6_spmd, %region_7.9_spmd} | conditional | flops 1101664256 | bytes 38933080 | solution.py:98
  196.3 2.5 fusion
  198.8 2.0 fusion.2
  200.8 2.9 fusion.6
  204.8 7.6 %conditional.5 = ((f32[4,4,128]{2,1,0:T(4,128)S(1)}, f32[4,4,128]{2,1,0:T(4,128)S(1)}, f32[4,4,128,128]{3,2,1,0:T(8,128)})) conditional(s32[]{:T(128)} %convert_element_type.39, (f32[4,4,128]{2,1,0:T(4,128)S(1)}, f32[4,4,128]{2,1,0:T(4,128)S(1)}, f32[4,4,128,128]{3,2,1,0:T(8,128)}) %tuple.59, (s32[1024]{0:T(1024)S(1)}, s32[128]{0:T(128)S(1)}, ...), branch_computations={%region_10.10_spmd, %region_11.13_spmd} | conditional | flops 1101664256 | bytes 38933080 | solution.py:98
  205.0 1.3 fusion.15
  206.3 2.0 fusion.17
  208.3 2.9 fusion.21
  216.5 1.8 constant_dynamic-slice_fusion.3
  219.6 8.7 %conditional.4 = ((f32[4,4,128]{2,1,0:T(4,128)S(1)}, f32[4,4,128]{2,1,0:T(4,128)S(1)}, f32[4,4,128,128]{3,2,1,0:T(8,128)})) conditional(s32[]{:T(128)} %convert_element_type.38, (f32[4,4,128]{2,1,0:T(4,128)S(1)}, f32[4,4,128]{2,1,0:T(4,128)S(1)}, f32[4,4,128,128]{3,2,1,0:T(8,128)}) %tuple.57, (s32[1024]{0:T(1024)S(1)}, s32[128]{0:T(128)S(1)}, ...), branch_computations={%region_6.6_spmd, %region_7.9_spmd} | conditional | flops 1101664256 | bytes 38933080 | solution.py:98
  219.9 2.5 fusion
  222.3 2.0 fusion.2
  224.4 2.9 fusion.6
  228.3 7.6 %conditional.5 = ((f32[4,4,128]{2,1,0:T(4,128)S(1)}, f32[4,4,128]{2,1,0:T(4,128)S(1)}, f32[4,4,128,128]{3,2,1,0:T(8,128)})) conditional(s32[]{:T(128)} %convert_element_type.39, (f32[4,4,128]{2,1,0:T(4,128)S(1)}, f32[4,4,128]{2,1,0:T(4,128)S(1)}, f32[4,4,128,128]{3,2,1,0:T(8,128)}) %tuple.59, (s32[1024]{0:T(1024)S(1)}, s32[128]{0:T(128)S(1)}, ...), branch_computations={%region_10.10_spmd, %region_11.13_spmd} | conditional | flops 1101664256 | bytes 38933080 | solution.py:98
  228.5 1.3 fusion.15
  229.8 2.0 fusion.17
  231.9 2.9 fusion.21
  240.0 1.8 constant_dynamic-slice_fusion.3
  243.1 8.7 %conditional.4 = ((f32[4,4,128]{2,1,0:T(4,128)S(1)}, f32[4,4,128]{2,1,0:T(4,128)S(1)}, f32[4,4,128,128]{3,2,1,0:T(8,128)})) conditional(s32[]{:T(128)} %convert_element_type.38, (f32[4,4,128]{2,1,0:T(4,128)S(1)}, f32[4,4,128]{2,1,0:T(4,128)S(1)}, f32[4,4,128,128]{3,2,1,0:T(8,128)}) %tuple.57, (s32[1024]{0:T(1024)S(1)}, s32[128]{0:T(128)S(1)}, ...), branch_computations={%region_6.6_spmd, %region_7.9_spmd} | conditional | flops 1101664256 | bytes 38933080 | solution.py:98
  243.4 2.5 fusion
  245.9 2.0 fusion.2
  247.9 2.9 fusion.6
  251.8 7.6 %conditional.5 = ((f32[4,4,128]{2,1,0:T(4,128)S(1)}, f32[4,4,128]{2,1,0:T(4,128)S(1)}, f32[4,4,128,128]{3,2,1,0:T(8,128)})) conditional(s32[]{:T(128)} %convert_element_type.39, (f32[4,4,128]{2,1,0:T(4,128)S(1)}, f32[4,4,128]{2,1,0:T(4,128)S(1)}, f32[4,4,128,128]{3,2,1,0:T(8,128)}) %tuple.59, (s32[1024]{0:T(1024)S(1)}, s32[128]{0:T(128)S(1)}, ...), branch_computations={%region_10.10_spmd, %region_11.13_spmd} | conditional | flops 1101664256 | bytes 38933080 | solution.py:98
  252.0 1.3 fusion.15
  253.4 2.0 fusion.17
  255.4 2.9 fusion.21
  263.5 1.8 constant_dynamic-slice_fusion.3
  266.7 8.7 %conditional.4 = ((f32[4,4,128]{2,1,0:T(4,128)S(1)}, f32[4,4,128]{2,1,0:T(4,128)S(1)}, f32[4,4,128,128]{3,2,1,0:T(8,128)})) conditional(s32[]{:T(128)} %convert_element_type.38, (f32[4,4,128]{2,1,0:T(4,128)S(1)}, f32[4,4,128]{2,1,0:T(4,128)S(1)}, f32[4,4,128,128]{3,2,1,0:T(8,128)}) %tuple.57, (s32[1024]{0:T(1024)S(1)}, s32[128]{0:T(128)S(1)}, ...), branch_computations={%region_6.6_spmd, %region_7.9_spmd} | conditional | flops 1101664256 | bytes 38933080 | solution.py:98
  266.9 2.5 fusion
  269.4 2.0 fusion.2
  271.4 2.9 fusion.6
  275.3 7.6 %conditional.5 = ((f32[4,4,128]{2,1,0:T(4,128)S(1)}, f32[4,4,128]{2,1,0:T(4,128)S(1)}, f32[4,4,128,128]{3,2,1,0:T(8,128)})) conditional(s32[]{:T(128)} %convert_element_type.39, (f32[4,4,128]{2,1,0:T(4,128)S(1)}, f32[4,4,128]{2,1,0:T(4,128)S(1)}, f32[4,4,128,128]{3,2,1,0:T(8,128)}) %tuple.59, (s32[1024]{0:T(1024)S(1)}, s32[128]{0:T(128)S(1)}, ...), branch_computations={%region_10.10_spmd, %region_11.13_spmd} | conditional | flops 1101664256 | bytes 38933080 | solution.py:98
  275.5 1.3 fusion.15
  276.9 2.0 fusion.17
  278.9 2.9 fusion.21
  282.9 2.1 divide_convert_fusion
  285.9 1.6 convert_element_type.24
  (122 shorter events, 25.9 us)
Async XLA Ops:
  6.5 23.0 %copy-start = (bf16[256,4096]{1,0:T(8,128)(2,1)S(1)}, bf16[256,4096]{1,0:T(8,128)(2,1)}, u32[]{:S(2)}) copy-start(bf16[256,4096]{1,0:T(8,128)(2,1)} %param.11) | copy-start | bytes 6291460
  6.5 180.0 %all-gather.2.cloned.1.call-start = ((), (), s32[]{:S(2)}) async-start(), calls=%async_computation | async-start | bytes 8912896 | tf_op jit(solution)/shard_map/all_gather | solution.py:55
  29.5 5.9 %slice-start = ((s8[8388608]{0:T(1024)(128)(4,1)}), s8[4194304]{0:T(1024)(128)(4,1)S(1)}, s32[]{:S(2)}) async-start(s8[8388608]{0:T(1024)(128)(4,1)} %bitcast.113), calls=%async_computation.1 | async-start | bytes 8388608
  29.5 5.9 %slice-start.1 = ((s8[8388608]{0:T(1024)(128)(4,1)}), s8[4194304]{0:T(1024)(128)(4,1)S(1)}, s32[]{:S(2)}) async-start(s8[8388608]{0:T(1024)(128)(4,1)} %bitcast.113), calls=%async_computation.2 | async-start | bytes 8388608
  35.5 11.9 %copy-start.8 = (u32[32]{0:T(128)S(1)}, u32[32]{0:T(128)}, u32[]{:S(2)}) copy-start(u32[32]{0:T(128)} %constant.81) | copy-start | bytes 388
  37.9 15.5 %copy-start.7 = (s32[32]{0:T(128)S(1)}, s32[32]{0:T(128)}, u32[]{:S(2)}) copy-start(s32[32]{0:T(128)} %param.15) | copy-start | bytes 388
  196.1 8.7 %copy-start.2 = (bf16[128,4,4,128]{3,0,2,1:T(8,128)(2,1)S(1)}, bf16[128,4,4,128]{3,0,2,1:T(8,128)(2,1)}, u32[]{:S(2)}) copy-start(bf16[128,4,4,128]{3,0,2,1:T(8,128)(2,1)} %get-tuple-element.466) | copy-start | bytes 1572868 | tf_op jit(solution)/shard_map/while
  196.3 4.5 %copy-start.5 = (f32[4,4,128,128]{3,2,1,0:T(8,128)S(1)}, f32[4,4,128,128]{3,2,1,0:T(8,128)}, u32[]{:S(2)}) copy-start(f32[4,4,128,128]{3,2,1,0:T(8,128)} %get-tuple-element.119) | copy-start | bytes 3145732 | tf_op jit(solution)/shard_map/while/body/eval_jaxpr/cond
  203.8 1.0 copy-start.6
  205.0 3.4 %copy-start.3 = (f32[4,4,128,128]{3,2,1,0:T(8,128)S(1)}, f32[4,4,128,128]{3,2,1,0:T(8,128)}, u32[]{:S(2)}) copy-start(f32[4,4,128,128]{3,2,1,0:T(8,128)} %get-tuple-element.127) | copy-start | bytes 3145732 | tf_op jit(solution)/shard_map/while/body/eval_jaxpr/cond
  211.3 1.0 copy-start.4
  219.6 8.7 %copy-start.2 = (bf16[128,4,4,128]{3,0,2,1:T(8,128)(2,1)S(1)}, bf16[128,4,4,128]{3,0,2,1:T(8,128)(2,1)}, u32[]{:S(2)}) copy-start(bf16[128,4,4,128]{3,0,2,1:T(8,128)(2,1)} %get-tuple-element.466) | copy-start | bytes 1572868 | tf_op jit(solution)/shard_map/while
  219.8 4.5 %copy-start.5 = (f32[4,4,128,128]{3,2,1,0:T(8,128)S(1)}, f32[4,4,128,128]{3,2,1,0:T(8,128)}, u32[]{:S(2)}) copy-start(f32[4,4,128,128]{3,2,1,0:T(8,128)} %get-tuple-element.119) | copy-start | bytes 3145732 | tf_op jit(solution)/shard_map/while/body/eval_jaxpr/cond
  227.3 1.0 copy-start.6
  228.5 3.4 %copy-start.3 = (f32[4,4,128,128]{3,2,1,0:T(8,128)S(1)}, f32[4,4,128,128]{3,2,1,0:T(8,128)}, u32[]{:S(2)}) copy-start(f32[4,4,128,128]{3,2,1,0:T(8,128)} %get-tuple-element.127) | copy-start | bytes 3145732 | tf_op jit(solution)/shard_map/while/body/eval_jaxpr/cond
  234.8 1.0 copy-start.4
  243.1 8.7 %copy-start.2 = (bf16[128,4,4,128]{3,0,2,1:T(8,128)(2,1)S(1)}, bf16[128,4,4,128]{3,0,2,1:T(8,128)(2,1)}, u32[]{:S(2)}) copy-start(bf16[128,4,4,128]{3,0,2,1:T(8,128)(2,1)} %get-tuple-element.466) | copy-start | bytes 1572868 | tf_op jit(solution)/shard_map/while
  243.4 4.5 %copy-start.5 = (f32[4,4,128,128]{3,2,1,0:T(8,128)S(1)}, f32[4,4,128,128]{3,2,1,0:T(8,128)}, u32[]{:S(2)}) copy-start(f32[4,4,128,128]{3,2,1,0:T(8,128)} %get-tuple-element.119) | copy-start | bytes 3145732 | tf_op jit(solution)/shard_map/while/body/eval_jaxpr/cond
  250.8 1.0 copy-start.6
  252.0 3.4 %copy-start.3 = (f32[4,4,128,128]{3,2,1,0:T(8,128)S(1)}, f32[4,4,128,128]{3,2,1,0:T(8,128)}, u32[]{:S(2)}) copy-start(f32[4,4,128,128]{3,2,1,0:T(8,128)} %get-tuple-element.127) | copy-start | bytes 3145732 | tf_op jit(solution)/shard_map/while/body/eval_jaxpr/cond
  258.3 1.0 copy-start.4
  266.6 8.7 %copy-start.2 = (bf16[128,4,4,128]{3,0,2,1:T(8,128)(2,1)S(1)}, bf16[128,4,4,128]{3,0,2,1:T(8,128)(2,1)}, u32[]{:S(2)}) copy-start(bf16[128,4,4,128]{3,0,2,1:T(8,128)(2,1)} %get-tuple-element.466) | copy-start | bytes 1572868 | tf_op jit(solution)/shard_map/while
  266.9 4.5 %copy-start.5 = (f32[4,4,128,128]{3,2,1,0:T(8,128)S(1)}, f32[4,4,128,128]{3,2,1,0:T(8,128)}, u32[]{:S(2)}) copy-start(f32[4,4,128,128]{3,2,1,0:T(8,128)} %get-tuple-element.119) | copy-start | bytes 3145732 | tf_op jit(solution)/shard_map/while/body/eval_jaxpr/cond
  274.3 1.0 copy-start.6
  275.5 3.4 %copy-start.3 = (f32[4,4,128,128]{3,2,1,0:T(8,128)S(1)}, f32[4,4,128,128]{3,2,1,0:T(8,128)}, u32[]{:S(2)}) copy-start(f32[4,4,128,128]{3,2,1,0:T(8,128)} %get-tuple-element.127) | copy-start | bytes 3145732 | tf_op jit(solution)/shard_map/while/body/eval_jaxpr/cond
  281.8 1.0 copy-start.4
  282.9 4.6 %copy-start.1 = (bf16[256,4096]{1,0:T(8,128)(2,1)S(1)}, bf16[256,4096]{1,0:T(8,128)(2,1)}, u32[]{:S(2)}) copy-start(bf16[256,4096]{1,0:T(8,128)(2,1)} %param.11) | copy-start | bytes 6291460
Sparse Core Ops, SparseCore 0:
  49.7 136.8 all-gather.1
where the time goes:
time: 295 us; the launch traced here: 294 us
  waiting for transfers between devices  132 us (45%)
  local copies, waits for them, and re-layouts  55.9 us (19%)
  matrix products  46.8 us (16%)
  other arithmetic  23.3 us (8%)
  between operations  14.2 us (5%)
  loops' own time  12.5 us (4%)
  blocking collectives  9.33 us (3%)
    all_gather x1, waiting for transfers between devices, body(): piece = lax.all_gather(kv_local, 'ctx', axis=0, tiled=True)  132 us
    dot_general x8, matrix products, attend(): jnp.einsum('grtn,ngd->grtd', weight.astype(jnp.bfloat16), value_block, pr...  23.4 us
    reduce_sum x8, other arithmetic, attend(): sums = sums * factor + jnp.sum(weight, axis=-1)  16 us
    dot_general x8, matrix products, attend(): jnp.einsum('tgrd,ngd->grtn', span_grid, key_block, preferred_element_type...  15 us
    another operation x1, loops' own time, body(): carry, _ = lax.scan(visit, carry, jnp.arange(blocks, dtype=jnp.int32))  11.9 us
    reshape x1, local copies, waits for them, and re-layouts, body(): key_matrix.reshape(key_matrix.shape[0], KEY_VALUE_HEADS, HEAD_SIZE)  11.7 us
    reshape x1, local copies, waits for them, and re-layouts, body(): value_matrix.reshape(value_matrix.shape[0], KEY_VALUE_HEADS, HEAD_SIZE)  11.3 us
    unnamed x1, blocking collectives  9.33 us
  transfers between devices with their start and end apart: 1, of which 1 were waited for; matrix products, arithmetic and copies ran while one was open for 2% of the time, Pallas kernels for 0%

commit v1 on v0

v1 whole, which is shorter than its diff:
```python
import functools

import jax
import jax.numpy as jnp
from jax import lax
from jax.experimental import pallas as pl
from jax.experimental.pallas import tpu as pltpu
from jax.sharding import PartitionSpec as P

KEY_VALUE_HEADS = 8
HEAD_SIZE = 128
D = HEAD_SIZE
ROWS = 256
NEG = -1e30
LOG2E = 1.4426950408889634
MESH = pl.DeviceIdType.MESH


def kernel(
    G, R, B, S,
    table, hid_hbm, q_hbm, wk_hbm, wv_hbm, out_hbm,
    hid, w, part_send, part_recv, stage, kv, q_buf, qs, kcat, vcat, acc, mx, ls, o_send,
    hid_sem, w_sem, part_ssem, part_rsem, a2a_ssem, kv_sem, ring_ssem, q_ssem, q_rsem, q_lsem,
    o_ssem, o_rsem, o_lsem,
):
    me = lax.axis_index("ctx")
    tp = lax.axis_index("tp")
    zi = me // G
    ji = me % G
    other = 1 - tp
    up = (zi + 1) % B * G + ji
    down = (zi + B - 1) % B * G + ji
    half_ring = B // 2
    qw = R * D

    order = list(range(1, G)) + [0]

    def fetch(n, k, group):
        col = pl.multiple_of((group * G + (ji + k) % G) * D, D)
        a = pltpu.make_async_copy(wk_hbm.at[:, pl.ds(col, D)], w.at[n, :, pl.ds(0, D)], w_sem.at[n, 0])
        b = pltpu.make_async_copy(wv_hbm.at[:, pl.ds(col, D)], w.at[n, :, pl.ds(D, D)], w_sem.at[n, 1])
        return a, b

    hid_copy = pltpu.make_async_copy(hid_hbm, hid, hid_sem)
    hid_copy.start()
    fetches = []
    for i, k in enumerate(order):
        for which in range(2):
            pair = fetch(2 * i + which, k, other if which == 0 else tp)
            pair[0].start()
            pair[1].start()
            fetches.append(pair)

    barrier = pltpu.get_barrier_semaphore()
    for k in range(1, G):
        pl.semaphore_signal(barrier, inc=1, device_id=(zi * G + (ji + k) % G, tp), device_id_type=MESH)
    pl.semaphore_signal(barrier, inc=1, device_id=(me, other), device_id_type=MESH)
    pl.semaphore_signal(barrier, inc=1, device_id=(up, tp), device_id_type=MESH)
    pl.semaphore_signal(barrier, inc=1, device_id=(down, tp), device_id_type=MESH)
    pl.semaphore_wait(barrier, G + 2)

    def q_copy(k, h):
        p = (ji + k) % G
        return pltpu.make_async_remote_copy(
            src_ref=q_hbm.at[pl.ds(h * S, S), pl.ds(pl.multiple_of(p * qw, qw), qw)],
            dst_ref=q_buf.at[ji, h],
            send_sem=q_ssem.at[k, h],
            recv_sem=q_rsem.at[k, h],
            device_id=(zi * G + p, tp),
            device_id_type=MESH,
        )

    def q_own(h):
        return pltpu.make_async_copy(
            q_hbm.at[pl.ds(h * S, S), pl.ds(pl.multiple_of(ji * qw, qw), qw)], q_buf.at[ji, h], q_lsem.at[h]
        )

    for h in range(2):
        q_own(h).start()
    q_copy(1, 0).start()
    q_copy(G - 1, 0).start()

    def ring_copy(z, j, s, way):
        return pltpu.make_async_remote_copy(
            src_ref=kv.at[z, j],
            dst_ref=kv.at[z, j],
            send_sem=ring_ssem.at[way, s, j],
            recv_sem=kv_sem.at[z, j],
            device_id=(up if way == 0 else down, tp),
            device_id_type=MESH,
        )

    def ring_send(z, j, s, way):
        if s < half_ring - 1:
            ring_copy(z, j, s, way).start()
        else:
            @pl.when((j < G // 2) if way == 0 else (j >= G // 2))
            def _():
                ring_copy(z, j, s, way).start()

    def ring_done(z, j, s, way):
        if s < half_ring - 1:
            ring_copy(z, j, s, way).wait_send()
        else:
            @pl.when((j < G // 2) if way == 0 else (j >= G // 2))
            def _():
                ring_copy(z, j, s, way).wait_send()

    def wait_piece(z, j):
        ring_copy(z, j, 0, 0).wait_recv()

    def part_copy(i):
        return pltpu.make_async_remote_copy(
            src_ref=part_send.at[i],
            dst_ref=part_recv.at[i],
            send_sem=part_ssem.at[i],
            recv_sem=part_rsem.at[i],
            device_id=(me, other),
            device_id_type=MESH,
        )

    def a2a_copy(i, k):
        return pltpu.make_async_remote_copy(
            src_ref=stage.at[i],
            dst_ref=kv.at[zi, ji],
            send_sem=a2a_ssem.at[i],
            recv_sem=kv_sem.at[zi, ji],
            device_id=(zi * G + (ji + k) % G, tp),
            device_id_type=MESH,
        )

    hid_copy.wait()
    for i, k in enumerate(order):
        for n in (2 * i, 2 * i + 1):
            fetches[n][0].wait()
            fetches[n][1].wait()
            term = jnp.dot(hid[...], w[n], preferred_element_type=jnp.float32)
            if n % 2 == 0:
                part_send[i] = term
                part_copy(i).start()
            else:
                part_copy(i).wait_recv()
                both = (term + part_recv[i]).astype(jnp.bfloat16)
                for c in range(2):
                    for h in range(2):
                        block = both[h * S:(h + 1) * S, c * D:(c + 1) * D]
                        if k:
                            stage[i, c, h] = block
                        else:
                            kv[zi, ji, c, h] = block
        if k:
            a2a_copy(i, k).start()
        if i == len(order) - 2:
            for kk in range(1, G):
                for h in range(2):
                    if not (h == 0 and kk in (1, G - 1)):
                        q_copy(kk, h).start()
        if i:
            j = (ji + G - order[i - 1]) % G
            wait_piece(zi, j)
            for way in range(2):
                ring_send(zi, j, 0, way)
        if not k:
            for way in range(2):
                ring_send(zi, ji, 0, way)

    def flipped(z, j):
        return table[2 * (z * G + j)] > table[2 * (z * G + j) + 1]

    def ids(z, j):
        a = table[2 * (z * G + j)]
        b = table[2 * (z * G + j) + 1]
        return jnp.minimum(a, b), jnp.maximum(a, b)

    def sort_queries(j):
        flip = flipped(zi, j)
        first = q_buf[j, 0]
        second = q_buf[j, 1]
        low = jnp.where(flip, second, first)
        high = jnp.where(flip, first, second)
        for r in range(R):
            qs[j, 0, r * S:(r + 1) * S] = low[:, r * D:(r + 1) * D]
            qs[j, 1, r * S:(r + 1) * S] = high[:, r * D:(r + 1) * D]

    for h in range(2):
        q_own(h).wait()
    sort_queries(ji)

    rows_all = R * S
    rows_at = min(ROWS, rows_all)
    scale2 = LOG2E / D**0.5

    def gather_group(z):
        for j in range(G):
            flip = flipped(z, j)
            for c, cat in ((0, kcat), (1, vcat)):
                first = kv[z, j, c, 0]
                second = kv[z, j, c, 1]
                cat[0, j * S:(j + 1) * S] = jnp.where(flip, second, first)
                cat[1, j * S:(j + 1) * S] = jnp.where(flip, first, second)

    def unit(z, jq, h, at, first):
        rows = pl.ds(pl.multiple_of(at * rows_at, rows_at), rows_at)
        qx = qs[jq, h, rows]
        tq = ids(zi, jq)[h]
        row = lax.broadcasted_iota(jnp.int32, (rows_at, S), 0) % S
        col = lax.broadcasted_iota(jnp.int32, (rows_at, S), 1)
        diff = col - row
        pieces = []
        for side in range(h + 1):
            s = lax.dot_general(
                qx, kcat[side], (((1,), (1,)), ((), ())), preferred_element_type=jnp.float32
            )
            for j in range(G):
                block = s[:, j * S:(j + 1) * S]
                if side == h:
                    tk = ids(z, j)[side]
                    block = jnp.where(diff <= (tq - tk) * S, block, jnp.float32(NEG))
                pieces.append(block)
        top = pieces[0]
        for block in pieces[1:]:
            top = jnp.maximum(top, block)
        top = jnp.max(top, axis=1, keepdims=True)
        if first:
            new = jnp.broadcast_to(top, (rows_at, D))
        else:
            old = mx[jq, h, rows]
            new = jnp.maximum(old, top)
        shift = new * scale2
        weights = [jnp.exp2(block * scale2 - shift) for block in pieces]
        total = weights[0]
        for weight in weights[1:]:
            total = total + weight
        value = None
        for side in range(h + 1):
            weight = jnp.concatenate(
                [x.astype(jnp.bfloat16) for x in weights[side * G:(side + 1) * G]], axis=1
            )
            term = jnp.dot(weight, vcat[side], preferred_element_type=jnp.float32)
            value = term if value is None else value + term
        if first:
            acc[jq, h, rows] = value
            ls[jq, h, rows] = total
        else:
            factor = jnp.exp2(old * scale2 - shift)
            acc[jq, h, rows] = acc[jq, h, rows] * factor + value
            ls[jq, h, rows] = ls[jq, h, rows] * factor + total
        mx[jq, h, rows] = new

    def visit_one(z, jq, first):
        def step(at, _):
            for h in range(2):
                unit(z, jq, h, at, first)
            return 0

        lax.fori_loop(0, rows_all // rows_at, step, 0)

    for h in range(2):
        pass
    gather_group(zi)
    visit_one(zi, ji, True)
    for k in range(1, G):
        for h in range(2):
            q_copy(k, h).wait_recv()
        sort_queries((ji + G - k) % G)

    def visit(z, first):
        def step(k, _):
            visit_one(z, (ji + k) % G, first)
            return 0

        lax.fori_loop(1 if first else 0, G, step, 0)

    visit(zi, True)

    for s in range(1, half_ring):
        below = (zi + B - s) % B
        above = (zi + s) % B
        if s < half_ring - 1:
            for j in range(G):
                wait_piece(below, j)
                ring_send(below, j, s, 0)
                wait_piece(above, j)
                ring_send(above, j, s, 1)
        else:
            for j in range(G // 2):
                wait_piece(below, j)
                ring_copy(below, j, s, 0).start()
                wait_piece(above, j + G // 2)
                ring_copy(above, j + G // 2, s, 1).start()
            for j in range(G // 2):
                wait_piece(below, j + G // 2)
        gather_group(below)
        visit(below, False)
        if s == half_ring - 1:
            for j in range(G // 2):
                wait_piece(above, j)
        gather_group(above)
        visit(above, False)

    def o_copy(k):
        p = (ji + k) % G
        return pltpu.make_async_remote_copy(
            src_ref=o_send.at[k],
            dst_ref=out_hbm.at[:, pl.ds(pl.multiple_of(ji * qw, qw), qw)],
            send_sem=o_ssem.at[k],
            recv_sem=o_rsem.at[k],
            device_id=(zi * G + p, tp),
            device_id_type=MESH,
        )

    last = (zi + half_ring) % B
    for j in range(G):
        wait_piece(last, j)
    gather_group(last)

    def finish(k):
        jq = (ji + k) % G
        visit_one(last, jq, False)
        flip = flipped(zi, jq)
        for r in range(R):
            rows = slice(r * S, (r + 1) * S)
            ends = [
                (acc[jq, h, rows] / jnp.sum(ls[jq, h, rows], axis=1, keepdims=True)).astype(jnp.bfloat16)
                for h in range(2)
            ]
            o_send[k, 0:S, r * D:(r + 1) * D] = jnp.where(flip, ends[1], ends[0])
            o_send[k, S:2 * S, r * D:(r + 1) * D] = jnp.where(flip, ends[0], ends[1])

    def finish_step(k, _):
        finish(k)
        o_copy(k).start()
        return 0

    lax.fori_loop(1, G, finish_step, 0)
    finish(0)
    mine = pltpu.make_async_copy(
        o_send.at[0], out_hbm.at[:, pl.ds(pl.multiple_of(ji * qw, qw), qw)], o_lsem
    )
    mine.start()

    for i, k in enumerate(order):
        part_copy(i).wait_send()
        if k:
            a2a_copy(i, k).wait_send()
            for h in range(2):
                q_copy(k, h).wait_send()
    for s in range(half_ring):
        for j in range(G):
            jj = (ji + j) % G
            ring_done((zi + B - s) % B, jj, s, 0)
            ring_done((zi + s) % B, jj, s, 1)
    for k in range(1, G):
        o_copy(k).wait_send()
        o_copy(k).wait_recv()
    mine.wait()


def body(hidden_states, queries, key_matrix, value_matrix, stretch_table):
    tokens, width = hidden_states.shape
    G = KEY_VALUE_HEADS // lax.axis_size("tp")
    ctx = lax.axis_size("ctx")
    B = ctx // G
    S = tokens // 2
    R = queries.shape[1] // (G * D)
    any_ = pl.BlockSpec(memory_space=pl.ANY)
    bf, f32 = jnp.bfloat16, jnp.float32
    dma = pltpu.SemaphoreType.DMA
    return pl.pallas_call(
        functools.partial(kernel, G, R, B, S),
        out_shape=jax.ShapeDtypeStruct(queries.shape, bf),
        in_specs=[pl.BlockSpec(memory_space=pltpu.SMEM)] + [any_] * 4,
        out_specs=any_,
        scratch_shapes=[
            pltpu.VMEM((tokens, width), bf),
            pltpu.VMEM((2 * G, width, 2 * D), bf),
            pltpu.VMEM((G, tokens, 2 * D), f32),
            pltpu.VMEM((G, tokens, 2 * D), f32),
            pltpu.VMEM((G, 2, 2, S, D), bf),
            pltpu.VMEM((B, G, 2, 2, S, D), bf),
            pltpu.VMEM((G, 2, S, R * D), bf),
            pltpu.VMEM((G, 2, R * S, D), bf),
            pltpu.VMEM((2, G * S, D), bf),
            pltpu.VMEM((2, G * S, D), bf),
            pltpu.VMEM((G, 2, R * S, D), f32),
            pltpu.VMEM((G, 2, R * S, D), f32),
            pltpu.VMEM((G, 2, R * S, D), f32),
            pltpu.VMEM((G, tokens, R * D), bf),
            dma,
            dma((2 * G, 2)),
            dma((G,)),
            dma((G,)),
            dma((G,)),
            dma((B, G)),
            dma((2, B // 2, G)),
            dma((G, 2)),
            dma((G, 2)),
            dma((2,)),
            dma((G,)),
            dma((G,)),
            dma,
        ],
        compiler_params=pltpu.CompilerParams(
            collective_id=0, has_side_effects=True, vmem_limit_bytes=60 * 1024 * 1024
        ),
        name="fused",
    )(stretch_table, hidden_states, queries, key_matrix, value_matrix)


def solution(mesh):
    in_specs = (P("ctx", "tp"), P("ctx", "tp"), P("tp", None), P("tp", None), P())
    out_specs = P("ctx", "tp")
    return jax.shard_map(body, mesh=mesh, in_specs=in_specs, out_specs=out_specs, check_vma=False)
```

time: 295 us -> 77.9 us (0.26)
  waiting for transfers between devices: 132 us -> 0 us
  Pallas kernels: 0 us -> 74.8 us
  local copies, waits for them, and re-layouts: 55.9 us -> 2.3 us
  matrix products: 46.8 us -> 0 us
  other arithmetic: 23.3 us -> 0 us
  between operations: 14.2 us -> 0.01 us
  loops' own time: 12.5 us -> 0 us
  blocking collectives: 9.33 us -> 0 us
    all_gather x1 -> x0, waiting for transfers between devices: 132 us -> none  [body(): piece = lax.all_gather(kv_local, 'ctx', axis=0, tiled=True)]
    pallas_call x0 -> x1, Pallas kernels: none -> 74.8 us  [body(): pl.pallas_call(functools.partial(kernel, G, R, B, S), out_shape=jax.Shape...]
    dot_general x18 -> x0, matrix products: 46.8 us -> none  [the longest x8 23.4 us: attend(): jnp.einsum('grtn,ngd->grtd', weight.astype(jnp.bfloat16), value_block, pr...]
    reshape x2 -> x0, local copies, waits for them, and re-layouts: 23 us -> none  [the longest x1 11.7 us: body(): key_matrix.reshape(key_matrix.shape[0], KEY_VALUE_HEADS, HEAD_SIZE)]
    reduce_sum x9 -> x0, other arithmetic: 16.2 us -> none  [the longest x8 16 us: attend(): sums = sums * factor + jnp.sum(weight, axis=-1)]
    another operation x9 -> x0, loops' own time: 12.5 us -> none  [the longest x1 11.9 us: body(): carry, _ = lax.scan(visit, carry, jnp.arange(blocks, dtype=jnp.int32))]
    unnamed x1 -> x0, blocking collectives: 9.33 us -> none
    slice x5 -> x0, local copies, waits for them, and re-layouts: 8.48 us -> none  [the longest x4 7.18 us: visit(): value_block = block[:, :, 1]]
  transfers between devices with their start and end apart: 1 -> 0, of which waited for: 1 -> 0; matrix products, arithmetic and copies ran while one was open for 2% -> 0% of each run, Pallas kernels for 0% -> 0%
where the time goes in v1:
time: 77.9 us; the launch traced here: 77.2 us
  Pallas kernels  74.8 us (96%)
  local copies, waits for them, and re-layouts  2.3 us (3%)
    pallas_call x1, Pallas kernels, body(): pl.pallas_call(functools.partial(kernel, G, R, B, S), out_shape=jax.Shape...  74.8 us
    unnamed x1, local copies, waits for them, and re-layouts  2.3 us

profile of v1, /device:TPU:0, one launch (start us, length us, event | category | flops | bytes accessed | tf_op | source)
XLA Modules:
  0.0 77.2 jit_solution(3418847899495092372)
XLA Ops:
  0.0 74.8 %fused.1 = bf16[256,2048]{1,0:T(8,128)(2,1)} custom-call(s32[32]{0:T(128)} %table.1, bf16[256,4096]{1,0:T(8,128)(2,1)} %hid_hbm.1, bf16[256,2048]{1,0:T(8,128)(2,1)} %q_hbm.1, bf16[4096,1024]{1,0:T(8,128)(2,1)} %wk_hbm.1, bf16[4096,1024]{1,0:T(8,128)(2,1)} %wv_hbm.1), custom_call_target="tpu_custom_call" | custom-call | tf_op jit(solution)/shard_map/fused/pallas_call | solution.py:369
  74.8 2.3 %copy.7 = bf16[256,2048]{1,0:T(8,128)(2,1)} copy(bf16[256,2048]{1,0:T(8,128)(2,1)} %fused.1) | data formatting | bytes 2097152

commit v2 on v1

--- a/solution.py
+++ b/solution.py
@@ -31,12 +31,16 @@
     up = (zi + 1) % B * G + ji
     down = (zi + B - 1) % B * G + ji
     half_ring = B // 2
+
+    def partner(k):
+        return (ji + k % 2 * (1 - 2 * (ji % 2)) + k - k % 2) % G
+
     qw = R * D
 
-    order = list(range(1, G)) + [0]
+    order = list(range(G - 1, -1, -1))
 
     def fetch(n, k, group):
-        col = pl.multiple_of((group * G + (ji + k) % G) * D, D)
+        col = pl.multiple_of((group * G + partner(k)) * D, D)
         a = pltpu.make_async_copy(wk_hbm.at[:, pl.ds(col, D)], w.at[n, :, pl.ds(0, D)], w_sem.at[n, 0])
         b = pltpu.make_async_copy(wv_hbm.at[:, pl.ds(col, D)], w.at[n, :, pl.ds(D, D)], w_sem.at[n, 1])
         return a, b
@@ -53,14 +57,14 @@
 
     barrier = pltpu.get_barrier_semaphore()
     for k in range(1, G):
-        pl.semaphore_signal(barrier, inc=1, device_id=(zi * G + (ji + k) % G, tp), device_id_type=MESH)
+        pl.semaphore_signal(barrier, inc=1, device_id=(zi * G + partner(k), tp), device_id_type=MESH)
     pl.semaphore_signal(barrier, inc=1, device_id=(me, other), device_id_type=MESH)
     pl.semaphore_signal(barrier, inc=1, device_id=(up, tp), device_id_type=MESH)
     pl.semaphore_signal(barrier, inc=1, device_id=(down, tp), device_id_type=MESH)
     pl.semaphore_wait(barrier, G + 2)
 
     def q_copy(k, h):
-        p = (ji + k) % G
+        p = partner(k)
         return pltpu.make_async_remote_copy(
             src_ref=q_hbm.at[pl.ds(h * S, S), pl.ds(pl.multiple_of(p * qw, qw), qw)],
             dst_ref=q_buf.at[ji, h],
@@ -78,7 +82,7 @@
     for h in range(2):
         q_own(h).start()
     q_copy(1, 0).start()
-    q_copy(G - 1, 0).start()
+    q_copy(2, 0).start()
 
     def ring_copy(z, j, s, way):
         return pltpu.make_async_remote_copy(
@@ -125,7 +129,7 @@
             dst_ref=kv.at[zi, ji],
             send_sem=a2a_ssem.at[i],
             recv_sem=kv_sem.at[zi, ji],
-            device_id=(zi * G + (ji + k) % G, tp),
+            device_id=(zi * G + partner(k), tp),
             device_id_type=MESH,
         )
 
@@ -153,10 +157,10 @@
         if i == len(order) - 2:
             for kk in range(1, G):
                 for h in range(2):
-                    if not (h == 0 and kk in (1, G - 1)):
+                    if not (h == 0 and kk in (1, 2)):
                         q_copy(kk, h).start()
         if i:
-            j = (ji + G - order[i - 1]) % G
+            j = partner(order[i - 1])
             wait_piece(zi, j)
             for way in range(2):
                 ring_send(zi, j, 0, way)
@@ -262,11 +266,11 @@
     for k in range(1, G):
         for h in range(2):
             q_copy(k, h).wait_recv()
-        sort_queries((ji + G - k) % G)
+        sort_queries(partner(k))
 
     def visit(z, first):
         def step(k, _):
-            visit_one(z, (ji + k) % G, first)
+            visit_one(z, partner(k), first)
             return 0
 
         lax.fori_loop(1 if first else 0, G, step, 0)
@@ -299,7 +303,7 @@
         visit(above, False)
 
     def o_copy(k):
-        p = (ji + k) % G
+        p = partner(k)
         return pltpu.make_async_remote_copy(
             src_ref=o_send.at[k],
             dst_ref=out_hbm.at[:, pl.ds(pl.multiple_of(ji * qw, qw), qw)],
@@ -315,7 +319,7 @@
     gather_group(last)
 
     def finish(k):
-        jq = (ji + k) % G
+        jq = partner(k)
         visit_one(last, jq, False)
         flip = flipped(zi, jq)
         for r in range(R):

time: 77.9 us -> 79.5 us (1.021)
  Pallas kernels: 74.8 us -> 77 us
    pallas_call x1, Pallas kernels: 74.8 us -> 77 us  [body(): pl.pallas_call(functools.partial(kernel, G, R, B, S), out_shape=jax.Shape...]
where the time goes in v2:
time: 79.5 us; the launch traced here: 79.3 us
  Pallas kernels  77 us (97%)
  local copies, waits for them, and re-layouts  2.3 us (3%)
    pallas_call x1, Pallas kernels, body(): pl.pallas_call(functools.partial(kernel, G, R, B, S), out_shape=jax.Shape...  77 us
    unnamed x1, local copies, waits for them, and re-layouts  2.3 us

profile of v2, /device:TPU:0, one launch (start us, length us, event | category | flops | bytes accessed | tf_op | source)
XLA Modules:
  0.0 79.3 jit_solution(17568233018784696841)
XLA Ops:
  0.0 77.0 %fused.1 = bf16[256,2048]{1,0:T(8,128)(2,1)} custom-call(s32[32]{0:T(128)} %table.1, bf16[256,4096]{1,0:T(8,128)(2,1)} %hid_hbm.1, bf16[256,2048]{1,0:T(8,128)(2,1)} %q_hbm.1, bf16[4096,1024]{1,0:T(8,128)(2,1)} %wk_hbm.1, bf16[4096,1024]{1,0:T(8,128)(2,1)} %wv_hbm.1), custom_call_target="tpu_custom_call" | custom-call | tf_op jit(solution)/shard_map/fused/pallas_call | solution.py:373
  77.0 2.3 %copy.7 = bf16[256,2048]{1,0:T(8,128)(2,1)} copy(bf16[256,2048]{1,0:T(8,128)(2,1)} %fused.1) | data formatting | bytes 2097152
